TPU v7x, 8 devices: a whole 2x2x1 slice. The times are simulated.
8 devices in a mesh: data: 8 (over z, y, x, core).
Axes of the slice: x: 2, y: 2, z: 1, core: 2. Of those that a mesh axis runs over, the one named last changes fastest.
Arguments:
- h_a: bfloat16 [8192, 512], P('data')
- h_b: bfloat16 [8192, 512], P('data')
- w_one: bfloat16 [512, 2048], replicated
- w_two: bfloat16 [2048, 2048], replicated
- w_three: bfloat16 [2048, 2048], replicated
- gain_one: float32 [2048], replicated
- bias_one: float32 [2048], replicated
- gain_two: float32 [2048], replicated
- bias_two: float32 [2048], replicated
Outputs:
- output 1: float32 [], replicated
- output 2: float32 [512, 2048], replicated
- output 3: float32 [2048, 2048], replicated
- output 4: float32 [2048, 2048], replicated
- output 5: float32 [2048], replicated
- output 6: float32 [2048], replicated
- output 7: float32 [2048], replicated
- output 8: float32 [2048], replicated
All inputs are finite; a program needn't handle non-finite values.
Results may differ from a plain program's by a relative error of at most 0.001.
Values are sent between devices in bfloat16 or wider.
A program may use at most 1 GiB of HBM per device.

v0:
```python
import functools

import jax
import jax.numpy as jnp
from jax import lax
from jax.experimental import pallas as pl
from jax.experimental.pallas import tpu as pltpu
from jax.sharding import PartitionSpec as P

BN_EPS = 1e-5
STD_EPS = 1e-4
INV_WEIGHT = 2.0
VAR_WEIGHT = 1.0
COV_WEIGHT = 2.0
BLK = 256

F32 = jnp.float32
BF16 = jnp.bfloat16


MESH_ID = pl.DeviceIdType.MESH


def remote(src, dst, send_sem, recv_sem, dev):
    return pltpu.make_async_remote_copy(src_ref=src, dst_ref=dst, send_sem=send_sem, recv_sem=recv_sem,
                                        device_id=(dev,), device_id_type=MESH_ID)


def meet(devs):
    barrier = pltpu.get_barrier_semaphore()
    for dev in devs:
        pl.semaphore_signal(barrier, inc=1, device_id=(dev,), device_id_type=MESH_ID)
    pl.semaphore_wait(barrier, len(devs))


def blk_ds(i):
    return pl.ds(pl.multiple_of(i * BLK, BLK), BLK)


def peer_of(idx, bits, d):
    dev = idx
    for b in range(3):
        if (d >> b) & 1:
            dev = dev + (1 << b) - (2 << b) * bits[b]
    return dev


def front_kernel(all_rows, ha_hbm, hb_hbm, w1_ref, w2_hbm, w3_hbm, vec_ref,
                 u1_hbm, x1_hbm, u2_hbm, z_hbm, zo_hbm, gh_hbm, x2t_hbm, x1t_hbm, ht_hbm,
                 stat1_ref, stat2_ref, mp_ref, loss_ref,
                 hbuf, wblk, xb, z, st, sr, zs, zs_all, mu_ref,
                 part, r1x, r1y, r2x, r2y, s2x, s2y, kx, ky, gb,
                 hsem, wsem, usem, xsem, osem, bsem, tsend, trecv, zsend, zrecv, osend, orecv, ssem, rsem):
    idx = lax.axis_index('data')
    c, x, y, q = idx % 2, (idx // 2) % 2, idx // 4, idx // 2
    bits = (c, x, y)
    nc, nx, ny = [peer_of(idx, bits, d) for d in (1, 2, 4)]
    chips = [peer_of(idx, bits, d) for d in (2, 4, 6)]
    rows, dim = z.shape
    half_rows = rows // 2
    half = BLK // 2
    lo, hi = pl.ds(0, half), pl.ds(half, half)
    tiles = [slice(0, half_rows), slice(half_rows, rows)]

    def start_all(cps):
        for cp in cps:
            cp.start()

    def wait_all(cps):
        for cp in cps:
            cp.wait()

    def views(what):
        for core, mine, other in ((0, ha_hbm, hb_hbm), (1, hb_hbm, ha_hbm)):
            @pl.when(c == core)
            def _():
                own = pltpu.make_async_copy(mine, hbuf.at[pl.ds(0, half_rows)], hsem.at[0])
                sent = remote(other, hbuf.at[pl.ds(half_rows, half_rows)], hsem.at[1], hsem.at[2], nc)
                if what == 'own':
                    own.start()
                elif what == 'send':
                    sent.start()
                    own.wait()
                else:
                    sent.wait()

    def w_copies(s):
        col = blk_ds(s % 8)
        return ((s < 16, pltpu.make_async_copy(w2_hbm.at[:, col], wblk.at[s % 2], wsem.at[s % 2])),
                (jnp.logical_and(s >= 16, s < 24),
                 pltpu.make_async_copy(w3_hbm.at[:, col], wblk.at[s % 2], wsem.at[s % 2])))

    def w_start(s):
        for cond, cp in w_copies(s):
            pl.when(cond)(cp.start)

    def columns(fn):
        def step(nb, carry):
            fn(nb, blk_ds(nb))
            return carry
        lax.fori_loop(0, dim // BLK, step, 0)

    def layers(u):
        def add_sums(layer, m, col, val):
            sums = jnp.concatenate([jnp.sum(val, axis=0, keepdims=True), jnp.sum(val * val, axis=0, keepdims=True)])
            st[layer, :, col] = sums if m == 0 else st[layer, :, col] + sums

        def statistics(layer, stat_ref):
            cps = [remote(st.at[layer], sr.at[layer, q], tsend.at[layer, i], trecv.at[layer, i], dev)
                   for i, dev in enumerate(chips)]
            start_all(cps)
            sr[layer, q] = st[layer]
            wait_all(cps)
            total = (sr[layer, 0] + sr[layer, 1]) + (sr[layer, 2] + sr[layer, 3])
            mean = total[0:1] / all_rows
            var = total[1:2] / all_rows - mean * mean
            stat_ref[0:1, :] = mean
            stat_ref[1:2, :] = lax.rsqrt(var + BN_EPS)
            stat_ref[2:4, :] = vec_ref[2 * layer:2 * layer + 2, :]

        def activate(stat_ref, m, col):
            nrm = (u[tiles[m], col] - stat_ref[0:1, col]) * stat_ref[1:2, col]
            xb[m, :, col] = jnp.maximum(stat_ref[2:3, col] * nrm + stat_ref[3:4, col], 0.0).astype(BF16)

        def u_out(layer, m):
            r = pl.ds(m * half_rows, half_rows)
            return pltpu.make_async_copy(u.at[r], (u1_hbm, u2_hbm)[layer].at[r], usem.at[m])

        def x_out(m):
            return pltpu.make_async_copy(xb.at[m], x1_hbm.at[pl.ds(m * half_rows, half_rows)], xsem.at[m])

        for m in range(2):
            if m == 1:
                views('got')

            def first(nb, col):
                val = jnp.dot(hbuf[tiles[m], :], w1_ref[:, col], preferred_element_type=F32)
                u[tiles[m], col] = val
                add_sums(0, m, col, val)
            columns(first)
            u_out(0, m).start()
        statistics(0, stat1_ref)

        columns(lambda nb, col: activate(stat1_ref, 0, col))
        for m in range(2):
            x_out(m).start()
            u_out(0, m).wait()

            def second(nb, col):
                s = 8 * m + nb
                w_copies(s)[0][1].wait()
                w_start(s + 1)
                val = jnp.dot(xb[m], wblk[s % 2], preferred_element_type=F32)
                if m == 0:
                    activate(stat1_ref, 1, col)
                u[tiles[m], col] = val
                add_sums(1, m, col, val)
            columns(second)
            u_out(1, m).start()
        statistics(1, stat2_ref)
        for m in range(2):
            x_out(m).wait()
            columns(lambda nb, col: activate(stat2_ref, m, col))
        for m in range(2):
            u_out(1, m).wait()

    views('own')
    w_start(0)
    meet([nc] + chips)
    views('send')
    pl.run_scoped(layers, pltpu.VMEM((rows, dim), F32))

    def block_of(o, g):
        b = 4 * g + o
        j = jnp.int32(0)
        for k in range(1, 8):
            j = j + jnp.where(b >= k * (k + 1) // 2, 1, 0)
        return b - j * (j + 1) // 2, j

    def s1(t):
        slot = t % 2
        return (remote(part.at[slot, :, 1 - x, lo, :], r1x.at[t], ssem.at[0, 0, t], rsem.at[0, 0, t], nx),
                remote(part.at[slot, 1 - y, :, hi, :], r1y.at[t], ssem.at[0, 1, t], rsem.at[0, 1, t], ny))

    def s2(t):
        slot = t % 2
        return (remote(s2x.at[slot], r2x.at[t], ssem.at[1, 0, t], rsem.at[1, 0, t], ny),
                remote(s2y.at[slot], r2y.at[t], ssem.at[1, 1, t], rsem.at[1, 1, t], nx))

    def a1(t):
        bx, by = gb.at[t, y, x, lo, :], gb.at[t, y, x, hi, :]
        return (remote(bx, bx, ssem.at[2, 0, t], rsem.at[2, 0, t], ny),
                remote(by, by, ssem.at[2, 1, t], rsem.at[2, 1, t], nx))

    def a2(t):
        bx, by = gb.at[t, :, x, lo, :], gb.at[t, y, :, hi, :]
        return (remote(bx, bx, ssem.at[3, 0, t], rsem.at[3, 0, t], nx),
                remote(by, by, ssem.at[3, 1, t], rsem.at[3, 1, t], ny))

    def z_sums(nb):
        return [remote(zs.at[nb], zs_all.at[q, nb], zsend.at[nb, i], zrecv.at[nb, i], dev)
                for i, dev in enumerate(chips)]

    def other_copies():
        first, second = pl.ds(0, half_rows), pl.ds(half_rows, half_rows)
        return [remote(z.at[second], zo_hbm.at[first], osend.at[0], orecv.at[0], nc),
                remote(z.at[first], zo_hbm.at[second], osend.at[1], orecv.at[1], nc),
                pltpu.make_async_copy(z, z_hbm, osem.at[0])]

    def gram(zt, gh, tin, tout, muc):
        mp_ref[...] = jnp.zeros_like(mp_ref)
        loss_ref[...] = jnp.zeros_like(loss_ref)

        def third(nb):
            col = blk_ds(nb)
            s = 16 + nb
            w_copies(s)[1][1].wait()
            w_start(s + 1)
            sums = jnp.zeros((1, BLK), F32)
            for m in range(2):
                val = jnp.dot(xb[m], wblk[s % 2], preferred_element_type=F32).astype(BF16)
                z[tiles[m], col] = val
                sums = sums + jnp.sum(val.astype(F32), axis=0, keepdims=True)
            zs[nb] = jnp.broadcast_to(sums, (8, BLK))
            start_all(z_sums(nb))
            zt[nb] = z[:, col].T

        def means(nb):
            wait_all(z_sums(nb))
            zs_all[q, nb] = zs[nb]
            total = (zs_all[0, nb] + zs_all[1, nb]) + (zs_all[2, nb] + zs_all[3, nb])
            mu = total[0:1] / all_rows
            mu_ref[:, blk_ds(nb)] = mu
            muc[blk_ds(nb), :] = jnp.broadcast_to(mu, (BLK, BLK)).T

        def each(lo_nb, hi_nb, fn):
            def step(nb, carry):
                fn(nb)
                return carry
            lax.fori_loop(lo_nb, hi_nb, step, 0)

        def new_col(t):
            return (jnp.logical_or(t < 4, jnp.logical_or(t == 5, t == 7)),
                    jnp.where(t < 4, t + 2, (t + 7) // 2))

        def x1_load(n):
            return pltpu.make_async_copy(x1_hbm.at[:, blk_ds(n)], tin, bsem.at[0])

        def store2(n):
            return pltpu.make_async_copy(tout.at[0], x2t_hbm.at[blk_ds(n), :], bsem.at[1])

        def store1(n):
            return pltpu.make_async_copy(tout.at[1], x1t_hbm.at[blk_ds(n), :], bsem.at[2])

        def store_h(n):
            return pltpu.make_async_copy(tout.at[n], ht_hbm.at[pl.ds(n * BLK, BLK), :], bsem.at[1 + n])

        each(0, 2, third)

        def body(t, carry):
            slot = t % 2
            old = (t + 1) % 2
            has_col, nb_new = new_col(t)

            @pl.when(jnp.logical_and(t >= 1, t < 9))
            def _():
                x1_load(t - 1).start()

            @pl.when(jnp.logical_and(t < 9, has_col))
            def _():
                third(nb_new)

            @pl.when(t == 7)
            def _():
                start_all(other_copies())

            @pl.when(t < 9)
            def _():
                for o in range(4):
                    i, j = block_of(o, t)
                    part[slot, o // 2, o % 2] = jnp.dot(zt[i], z[:, blk_ds(j)], preferred_element_type=F32)
                start_all(s1(t))

            @pl.when(jnp.logical_and(t >= 1, t < 10))
            def _():
                g = t - 1
                wait_all(s1(g))
                s2x[old] = part[old, 1 - y, x, lo, :] + r1x[g, 1 - y]
                s2y[old] = part[old, y, 1 - x, hi, :] + r1y[g, 1 - x]
                start_all(s2(g))
                kx[old] = part[old, y, x, lo, :] + r1x[g, y]
                ky[old] = part[old, y, x, hi, :] + r1y[g, x]

            @pl.when(jnp.logical_and(t >= 2, t < 11))
            def _():
                g = t - 2
                had_col, nb_old = new_col(g)

                @pl.when(g == 0)
                def _():
                    each(0, 2, means)

                @pl.when(had_col)
                def _():
                    means(nb_old)

                wait_all(s2(g))
                i, j = block_of(q, g)
                mu_j = mu_ref[:, blk_ds(j)]
                on_diag = i == j
                r_i = lax.broadcasted_iota(jnp.int32, (half, BLK), 0)
                k_i = lax.broadcasted_iota(jnp.int32, (half, BLK), 1)
                for off, k_ref, r_ref in ((0, kx, r2x), (half, ky, r2y)):
                    mu_i = muc[pl.ds(pl.multiple_of(i * BLK + off, half), half), :]
                    cov = (k_ref[slot] + r_ref[g] - all_rows * (mu_i * mu_j)) / (all_rows - 1)
                    diag = jnp.logical_and(r_i + off == k_i, on_diag)
                    std = jnp.sqrt(jnp.where(diag, cov, 1.0) + STD_EPS)
                    g_diag = jnp.where(std < 1.0, -VAR_WEIGHT, 0.0) / (2.0 * std)
                    g_val = jnp.where(diag, g_diag, (2.0 * COV_WEIGHT) * cov)
                    gb[g, y, x, pl.ds(off, half), :] = g_val.astype(BF16)
                    weight = jnp.where(on_diag, COV_WEIGHT, 2.0 * COV_WEIGHT)
                    terms = jnp.where(diag, VAR_WEIGHT * jnp.maximum(1.0 - std, 0.0), weight * cov * cov)
                    loss_ref[...] += jnp.sum(terms, axis=0, keepdims=True)
                start_all(a1(g))

            @pl.when(jnp.logical_and(t >= 3, t < 12))
            def _():
                wait_all(a1(t - 3))
                start_all(a2(t - 3))

            @pl.when(jnp.logical_and(t >= 2, t < 10))
            def _():
                store2(t - 2).wait()
                store1(t - 2).wait()

            @pl.when(jnp.logical_and(t >= 1, t < 9))
            def _():
                band = blk_ds(t - 1)
                for m in range(2):
                    tout[0, :, tiles[m]] = xb[m, :, band].T
                store2(t - 1).start()
                x1_load(t - 1).wait()
                tout[1] = tin[...].T
                store1(t - 1).start()

            @pl.when(t == 9)
            def _():
                for n in range(2):
                    tout[n] = hbuf[:, n * BLK:(n + 1) * BLK].T
                    store_h(n).start()

            @pl.when(t >= 4)
            def _():
                g = t - 4
                wait_all(a2(g))
                for o in range(4):
                    i, j = block_of(o, g)
                    blk = gb[g, o // 2, o % 2]
                    gh[blk_ds(i), blk_ds(j)] = blk
                    mp_ref[:, blk_ds(j)] += jnp.sum(muc[blk_ds(i), :] * blk.astype(F32), axis=0, keepdims=True)

                    @pl.when(i != j)
                    def _():
                        blk_t = gb[g, o // 2, o % 2].T
                        gh[blk_ds(j), blk_ds(i)] = blk_t
                        mp_ref[:, blk_ds(i)] += jnp.sum(muc[blk_ds(j), :] * blk_t.astype(F32), axis=0, keepdims=True)

            return carry

        lax.fori_loop(0, 13, body, 0)
        gh_out = pltpu.make_async_copy(gh, gh_hbm, osem.at[1])
        gh_out.start()
        for n in range(2):
            store_h(n).wait()
        wait_all(other_copies())
        gh_out.wait()

    pl.run_scoped(gram, pltpu.VMEM((8, BLK, rows), BF16), pltpu.VMEM((dim, dim), BF16), pltpu.VMEM((rows, BLK), BF16),
                  pltpu.VMEM((2, BLK, rows), BF16), pltpu.VMEM((dim, BLK), F32))


def front(h_a, h_b, w1, w2, w3, vec, all_rows):
    rows, feat = 2 * h_a.shape[0], h_a.shape[1]
    dim = w2.shape[0]
    half = BLK // 2
    hbm = pl.BlockSpec(memory_space=pl.ANY)
    vmem = pl.BlockSpec(memory_space=pltpu.VMEM)
    dma = pltpu.SemaphoreType.DMA
    shape = jax.ShapeDtypeStruct
    return pl.pallas_call(
        functools.partial(front_kernel, all_rows),
        out_shape=(shape((rows, dim), F32), shape((rows, dim), BF16), shape((rows, dim), F32),
                   shape((rows, dim), BF16), shape((rows, dim), BF16), shape((dim, dim), BF16),
                   shape((dim, rows), BF16), shape((dim, rows), BF16), shape((feat, rows), BF16),
                   shape((4, dim), F32), shape((4, dim), F32), shape((1, dim), F32), shape((1, BLK), F32)),
        in_specs=[hbm, hbm, vmem, hbm, hbm, vmem],
        out_specs=(hbm,) * 9 + (vmem,) * 4,
        scratch_shapes=[
            pltpu.VMEM((rows, feat), BF16), pltpu.VMEM((2, dim, BLK), BF16),
            pltpu.VMEM((2, rows // 2, dim), BF16), pltpu.VMEM((rows, dim), BF16),
            pltpu.VMEM((2, 2, dim), F32), pltpu.VMEM((2, 4, 2, dim), F32),
            pltpu.VMEM((8, 8, BLK), F32), pltpu.VMEM((4, 8, 8, BLK), F32), pltpu.VMEM((1, dim), F32),
            pltpu.VMEM((2, 2, 2, BLK, BLK), F32),
            pltpu.VMEM((9, 2, half, BLK), F32), pltpu.VMEM((9, 2, half, BLK), F32),
            pltpu.VMEM((9, half, BLK), F32), pltpu.VMEM((9, half, BLK), F32),
            pltpu.VMEM((2, half, BLK), F32), pltpu.VMEM((2, half, BLK), F32),
            pltpu.VMEM((2, half, BLK), F32), pltpu.VMEM((2, half, BLK), F32),
            pltpu.VMEM((9, 2, 2, BLK, BLK), BF16),
            dma((3,)), dma((2,)), dma((2,)), dma((2,)), dma((2,)), dma((3,)), dma((2, 3)), dma((2, 3)),
            dma((8, 3)), dma((8, 3)), dma((2,)), dma((2,)), dma((4, 2, 9)), dma((4, 2, 9)),
        ],
        compiler_params=pltpu.CompilerParams(collective_id=3, has_side_effects=True, vmem_limit_bytes=67043328),
        cost_estimate=pl.CostEstimate(flops=50 * 10 ** 9, bytes_accessed=120 << 20, transcendentals=0),
    )(h_a, h_b, w1, w2, w3, vec)


LAG = 2
SLOTS = 6 * LAG
LANE = 128
GROUPS = 36
TILE = 1024


def backward_kernel(all_rows, z_hbm, zo_hbm, gh_hbm, x2t_hbm, x1t_hbm, ht_hbm, w3_hbm, w2_hbm, u2_hbm, u1_hbm,
                    mp_ref, vec2_ref, vec1_ref, lossv_ref,
                    out_hbm, part_hbm, grads_ref, loss_ref,
                    buf_a, buf_b, buf_c, ht, sb, wb, zb, ub, ps, own, r0, r1, r2, st, sr, tot, lacc,
                    ssem, rsem, lsem, dsem, psem, bsem, tsend, trecv):
    idx = lax.axis_index('data')
    c, x, y = idx % 2, (idx // 2) % 2, idx // 4
    bits = (c, x, y)

    def peer(d):
        dev = idx
        for b in range(3):
            if (d >> b) & 1:
                dev = dev + (1 << b) - (2 << b) * bits[b]
        return dev

    nc, nx, ny = peer(1), peer(2), peer(4)
    dim = buf_a.shape[1]
    rows = buf_a.shape[0]

    def rds(start, size):
        return pl.ds(pl.multiple_of(start, size), size)

    row_x, row_y = x * 256 + y * 128, 512 + y * 256 + x * 128

    def s0(g):
        k = g % SLOTS
        return (remote(part_hbm.at[g, rds((1 - c) * 1024, 1024)], r0.at[k], ssem.at[0, k], rsem.at[0, k], nc),)

    def load_own(g):
        k = g % SLOTS
        return pltpu.make_async_copy(part_hbm.at[g, rds(c * 1024, 1024)], own.at[k], lsem.at[0, k])

    def s1(g):
        k = g % SLOTS
        return (remote(own.at[k, rds((1 - x) * 256, 256)], r1.at[0, k], ssem.at[1, k], rsem.at[1, k], nx),
                remote(own.at[k, rds(512 + (1 - y) * 256, 256)], r1.at[1, k], ssem.at[2, k], rsem.at[2, k], ny))

    def s2(g):
        k = g % SLOTS
        return (remote(own.at[k, rds(x * 256 + (1 - y) * 128, 128)], r2.at[0, k], ssem.at[3, k], rsem.at[3, k], ny),
                remote(own.at[k, rds(512 + y * 256 + (1 - x) * 128, 128)], r2.at[1, k], ssem.at[4, k], rsem.at[4, k],
                       nx))

    def a1(g):
        k = g % SLOTS
        ox, oy = out_hbm.at[g, rds(c * 1024 + row_x, 128)], out_hbm.at[g, rds(c * 1024 + row_y, 128)]
        return (remote(own.at[k, rds(row_x, 128)], ox, ssem.at[5, k], rsem.at[5, k], ny),
                remote(own.at[k, rds(row_y, 128)], oy, ssem.at[6, k], rsem.at[6, k], nx),
                pltpu.make_async_copy(own.at[k, rds(row_x, 128)], ox, lsem.at[1, k]),
                pltpu.make_async_copy(own.at[k, rds(row_y, 128)], oy, lsem.at[2, k]))

    def a2(g):
        k = g % SLOTS
        bx, by = out_hbm.at[g, rds(c * 1024 + x * 256, 256)], out_hbm.at[g, rds(c * 1024 + 512 + y * 256, 256)]
        return (remote(bx, bx, ssem.at[7, k], rsem.at[7, k], nx), remote(by, by, ssem.at[8, k], rsem.at[8, k], ny))

    def a0(g):
        k = g % SLOTS
        b = out_hbm.at[g, rds(c * 1024, 1024)]
        return (remote(b, b, ssem.at[9, k], rsem.at[9, k], nc),)

    def stage(g, fn):
        @pl.when(jnp.logical_and(g >= 0, g < GROUPS))
        def _():
            fn(g)

    def wait_all(cps):
        for cp in cps:
            cp.wait()

    def start_all(cps):
        for cp in cps:
            cp.start()

    def to_a0(g):
        wait_all(a2(g))
        start_all(a0(g))

    def to_a2(g):
        wait_all(a1(g))
        start_all(a2(g))

    def to_a1(g):
        wait_all(s2(g))
        k = g % SLOTS
        own[k, rds(row_x, 128)] += r2[0, k]
        own[k, rds(row_y, 128)] += r2[1, k]
        start_all(a1(g))

    def to_s2(g):
        wait_all(s1(g))
        k = g % SLOTS
        own[k, rds(x * 256, 256)] += r1[0, k]
        own[k, rds(512 + y * 256, 256)] += r1[1, k]
        start_all(s2(g))

    def to_s1(g):
        wait_all(s0(g))
        load_own(g).wait()
        k = g % SLOTS
        own[k] += r0[k]
        start_all(s1(g))

    def to_s0(g):
        start_all(s0(g))
        load_own(g).start()

    def streams(n):
        slot = n % 2
        blk = n % 8
        return ((n < 8, (pltpu.make_async_copy(gh_hbm.at[:, blk_ds(blk)], sb.at[slot], dsem.at[0, slot]),
                         pltpu.make_async_copy(zo_hbm.at[:, blk_ds(blk)], zb.at[slot], dsem.at[1, slot]))),
                (jnp.logical_and(n >= 8, n < 24),
                 (pltpu.make_async_copy(w3_hbm.at[blk_ds(blk), :], wb.at[slot], dsem.at[0, slot]),
                  pltpu.make_async_copy(u2_hbm.at[:, blk_ds(blk)], ub.at[slot], dsem.at[1, slot]))),
                (jnp.logical_and(n >= 24, n < 40),
                 (pltpu.make_async_copy(w2_hbm.at[blk_ds(blk), :], wb.at[slot], dsem.at[0, slot]),
                  pltpu.make_async_copy(u1_hbm.at[:, blk_ds(blk)], ub.at[slot], dsem.at[1, slot]))))

    def start_streams(n):
        for cond, cps in streams(n):
            pl.when(cond)(functools.partial(start_all, cps))

    def wait_streams(n, which):
        wait_all(streams(n)[which][1])

    def part_writes(n):
        g = jnp.where(n < 8, 2 * n, 2 * n - 16)
        return tuple(pltpu.make_async_copy(ps.at[:, pl.ds(h * LANE, LANE)], part_hbm.at[g + h], psem.at[h])
                     for h in range(2))

    def part_writes_one(n):
        tile = 2 * (n - 32)
        return tuple(pltpu.make_async_copy(ps.at[pl.ds(0, 512), pl.ds(h * LANE, LANE)],
                                           part_hbm.at[32 + (tile + h) // 4, rds(((tile + h) % 4) * 512, 512)],
                                           psem.at[h]) for h in range(2))

    def loop_tiles(count, fn):
        def step(m, carry):
            fn(pl.ds(pl.multiple_of(m * TILE, TILE), TILE))
            return carry
        lax.fori_loop(0, count, step, 0)

    def nt(a, b):
        return lax.dot_general(a, b, (((1,), (1,)), ((), ())), preferred_element_type=F32)

    def piece_dz(n):
        slot, col = n % 2, blk_ds(n % 8)
        wait_streams(n, 0)
        start_streams(n + 1)

        def tile(r):
            rp = jnp.dot(buf_a[r, :], sb[slot], preferred_element_type=F32)
            zd = buf_a[r, col].astype(F32) - zb[slot, r, :].astype(F32)
            dz = (2.0 / (all_rows - 1)) * (rp - mp_ref[:, col]) + (2.0 * INV_WEIGHT / all_rows) * zd
            buf_c[r, col] = dz.astype(BF16)
            lacc[...] += jnp.sum(zd * zd, axis=0, keepdims=True)
        loop_tiles(rows // TILE, tile)

        @pl.when(n == 0)
        def _():
            big(1).wait()

        def grad(r):
            ps[r, :] = jnp.dot(buf_b[r, :], buf_c[:, col], preferred_element_type=F32)
        loop_tiles(dim // TILE, grad)
        start_all(part_writes(n))

    def d_act(d_ref, u_slot, r, vec_ref, col, slot):
        dx = nt(d_ref[r, :], wb[slot])
        nrm = (ub[slot, r, :] - vec_ref[0:1, col]) * vec_ref[1:2, col]
        act = vec_ref[2:3, col] * nrm + vec_ref[3:4, col]
        return jnp.where(act > 0.0, dx, 0.0), nrm

    def piece_stats(n, d_ref, vec_ref, layer, which):
        slot, col = n % 2, blk_ds(n % 8)
        wait_streams(n, which)
        start_streams(n + 1)
        st[layer, 0:2, col] = jnp.zeros((2, BLK), F32)

        def tile(r):
            da, nrm = d_act(d_ref, slot, r, vec_ref, col, slot)
            st[layer, 0:1, col] += jnp.sum(da, axis=0, keepdims=True)
            st[layer, 1:2, col] += jnp.sum(da * nrm, axis=0, keepdims=True)
        loop_tiles(rows // TILE, tile)

    def piece_du(n, d_ref, vec_ref, layer, which, du_ref):
        slot, col = n % 2, blk_ds(n % 8)
        wait_streams(n, which)
        start_streams(n + 1)

        def tile(r):
            da, nrm = d_act(d_ref, slot, r, vec_ref, col, slot)
            du = (vec_ref[1:2, col] * vec_ref[2:3, col]) * (
                da - tot[layer, 0:1, col] / all_rows - nrm * (tot[layer, 1:2, col] / all_rows))
            du_ref[r, col] = du.astype(BF16)
        loop_tiles(rows // TILE, tile)
        return col

    def stat_copies(layer):
        return tuple(remote(st.at[layer], sr.at[layer, idx], tsend.at[layer, d - 1], trecv.at[layer, d - 1], peer(d))
                     for d in range(1, 8))

    def send_stats(layer):
        start_all(stat_copies(layer))

    def finish_stats(layer):
        wait_all(stat_copies(layer))
        sr[layer, idx] = st[layer]
        va = (sr[layer, 0] + sr[layer, 2]) + (sr[layer, 4] + sr[layer, 6])
        vb = (sr[layer, 1] + sr[layer, 3]) + (sr[layer, 5] + sr[layer, 7])
        tot[layer] = jnp.where(c == 0, va, vb)
        grads_ref[layer] = va + vb

    def big(i):
        src = (z_hbm, x2t_hbm, x1t_hbm)[i]
        return pltpu.make_async_copy(src, (buf_a, buf_b, buf_a)[i], bsem.at[i])

    big(0).start()
    start_streams(0)
    big(1).start()
    ht_copy = pltpu.make_async_copy(ht_hbm, ht, bsem.at[3])
    ht_copy.start()
    lacc[...] = jnp.zeros_like(lacc)
    st[...] = jnp.zeros_like(st)
    meet([peer(d) for d in range(1, 8)])
    big(0).wait()

    def tick(it, carry):
        k = it - 1
        stage(k - 6 * LAG, lambda g: wait_all(a0(g)))
        stage(k - 5 * LAG, to_a0)
        stage(k - 4 * LAG, to_a2)
        stage(k - 3 * LAG, to_a1)
        stage(k - 2 * LAG, to_s2)
        stage(k - LAG, to_s1)

        @pl.when(jnp.logical_or(jnp.logical_and(it >= 1, it <= 8), jnp.logical_and(it >= 17, it <= 24)))
        def _():
            wait_all(part_writes(it - 1))

        @pl.when(jnp.logical_and(it >= 29, it <= 36))
        def _():
            wait_all(part_writes_one(it + 3))

        stage(k, to_s0)

        @pl.when(it < 8)
        def _():
            piece_dz(it)

        @pl.when(jnp.logical_and(it >= 8, it < 16))
        def _():
            @pl.when(it == 8)
            def _():
                big(2).start()

            piece_stats(it, buf_c, vec2_ref, 0, 1)

            @pl.when(it == 15)
            def _():
                st[0, 2:3, 0:BLK] = lossv_ref[...] + lacc[...] * (0.5 * INV_WEIGHT / all_rows)
                send_stats(0)

        @pl.when(jnp.logical_and(it >= 16, it < 24))
        def _():
            @pl.when(it == 16)
            def _():
                finish_stats(0)
                loss_ref[...] = jnp.broadcast_to(jnp.sum(grads_ref[0, 2:3, 0:BLK], axis=1, keepdims=True),
                                                 loss_ref.shape)
                big(2).wait()
                ht_copy.wait()

            col = piece_du(it, buf_c, vec2_ref, 0, 1, buf_b)

            def grad(r):
                ps[r, :] = jnp.dot(buf_a[r, :], buf_b[:, col], preferred_element_type=F32)
            loop_tiles(dim // TILE, grad)
            start_all(part_writes(it))

        @pl.when(jnp.logical_and(it >= 24, it < 28))
        def _():
            def two(m, carry):
                piece_stats(24 + 2 * (it - 24) + m, buf_b, vec1_ref, 1, 2)
                return carry
            lax.fori_loop(0, 2, two, 0)

            @pl.when(it == 27)
            def _():
                send_stats(1)

        @pl.when(jnp.logical_and(it >= 28, it < 36))
        def _():
            @pl.when(it == 28)
            def _():
                finish_stats(1)

            n = it + 4
            col = piece_du(n, buf_b, vec1_ref, 1, 2, buf_c)
            ps[0:512, :] = jnp.dot(ht[...], buf_c[:, col], preferred_element_type=F32)
            start_all(part_writes_one(n))

        return carry

    lax.fori_loop(0, GROUPS + 1 + 6 * LAG, tick, 0)


def backward(z, zo, gh, x2t, x1t, ht, w3, w2, u2, u1, mp, vec2, vec1, lossv, all_rows):
    rows, dim = z.shape
    feat = ht.shape[0]
    hbm = pl.BlockSpec(memory_space=pl.ANY)
    vmem = pl.BlockSpec(memory_space=pltpu.VMEM)
    dma = pltpu.SemaphoreType.DMA
    return pl.pallas_call(
        functools.partial(backward_kernel, all_rows),
        out_shape=(jax.ShapeDtypeStruct((GROUPS, dim, LANE), F32), jax.ShapeDtypeStruct((GROUPS, dim, LANE), F32),
                   jax.ShapeDtypeStruct((2, 4, dim), F32), jax.ShapeDtypeStruct((1, LANE), F32)),
        in_specs=[hbm] * 10 + [vmem] * 4,
        out_specs=(hbm, hbm, vmem, vmem),
        scratch_shapes=[
            pltpu.VMEM((rows, dim), BF16), pltpu.VMEM((rows, dim), BF16), pltpu.VMEM((rows, dim), BF16),
            pltpu.VMEM((feat, rows), BF16),
            pltpu.VMEM((2, dim, BLK), BF16), pltpu.VMEM((2, BLK, dim), BF16), pltpu.VMEM((2, rows, BLK), BF16),
            pltpu.VMEM((2, rows, BLK), F32), pltpu.VMEM((dim, BLK), F32),
            pltpu.VMEM((SLOTS, 1024, LANE), F32), pltpu.VMEM((SLOTS, 1024, LANE), F32),
            pltpu.VMEM((2, SLOTS, 256, LANE), F32), pltpu.VMEM((2, SLOTS, 128, LANE), F32),
            pltpu.VMEM((2, 4, dim), F32), pltpu.VMEM((2, 8, 4, dim), F32), pltpu.VMEM((2, 4, dim), F32),
            pltpu.VMEM((1, BLK), F32),
            dma((10, SLOTS)), dma((10, SLOTS)), dma((3, SLOTS)), dma((2, 2)), dma((2,)), dma((4,)),
            dma((2, 7)), dma((2, 7)),
        ],
        compiler_params=pltpu.CompilerParams(collective_id=2, has_side_effects=True, vmem_limit_bytes=67043328),
        cost_estimate=pl.CostEstimate(flops=150 * 10 ** 9, bytes_accessed=200 << 20, transcendentals=0),
    )(z, zo, gh, x2t, x1t, ht, w3, w2, u2, u1, mp, vec2, vec1, lossv)


RING = 16
AHEAD = 8


def join_kernel(groups, w1_out, w2_out, w3_out, buf, lsem, ssem):
    def load(g):
        return pltpu.make_async_copy(groups.at[g], buf.at[g % RING], lsem.at[g % RING])

    def stores(g):
        k = g % RING
        if g < 32:
            out = (w3_out, w2_out)[g // 16]
            return [pltpu.make_async_copy(buf.at[k], out.at[:, pl.ds((g % 16) * LANE, LANE)], ssem.at[k, 0])]
        return [pltpu.make_async_copy(buf.at[k, pl.ds(i * 512, 512)],
                                      w1_out.at[:, pl.ds(((g - 32) * 4 + i) * LANE, LANE)], ssem.at[k, i])
                for i in range(4)]

    for g in range(AHEAD):
        load(g).start()
    for g in range(GROUPS):
        load(g).wait()
        for cp in stores(g):
            cp.start()
        n = g + AHEAD
        if n < GROUPS:
            if n >= RING:
                for cp in stores(n - RING):
                    cp.wait()
            load(n).start()
    for g in range(GROUPS - RING, GROUPS):
        for cp in stores(g):
            cp.wait()


def join(groups, dim):
    hbm = pl.BlockSpec(memory_space=pl.ANY)
    return pl.pallas_call(
        join_kernel,
        out_shape=(jax.ShapeDtypeStruct((512, dim), F32), jax.ShapeDtypeStruct((dim, dim), F32),
                   jax.ShapeDtypeStruct((dim, dim), F32)),
        in_specs=[hbm],
        out_specs=(hbm, hbm, hbm),
        scratch_shapes=[pltpu.VMEM((RING, dim, LANE), F32), pltpu.SemaphoreType.DMA((RING,)),
                        pltpu.SemaphoreType.DMA((RING, 4))],
        compiler_params=pltpu.CompilerParams(vmem_limit_bytes=40 << 20),
        cost_estimate=pl.CostEstimate(flops=0, bytes_accessed=8 * GROUPS * dim * LANE, transcendentals=0),
    )(groups)


def solution(mesh):
    group_devs = mesh.shape['data']

    def local_step(h_a, h_b, w_one, w_two, w_three, gain_one, bias_one, gain_two, bias_two):
        all_rows = h_a.shape[0] * group_devs
        dim = w_two.shape[0]
        vec = jnp.stack([gain_one, bias_one, gain_two, bias_two])
        (u1, _, u2, z, z_other, g_hat, x2t, x1t, ht, stat1, stat2, mean_part, loss_vec) = front(
            h_a, h_b, w_one, w_two, w_three, vec, all_rows)
        groups, _, grads, loss = backward(z, z_other, g_hat, x2t, x1t, ht, w_three, w_two, u2, u1, mean_part, stat2,
                                          stat1, loss_vec, all_rows)
        d_w1, d_w2, d_w3 = join(groups, dim)
        return (loss[0, 0], d_w1, d_w2, d_w3,
                grads[1, 1], grads[1, 0], grads[0, 1], grads[0, 0])

    row_spec = P('data', None)
    return jax.shard_map(local_step, mesh=mesh,
                         in_specs=(row_spec, row_spec, P(), P(), P(), P(), P(), P(), P()),
                         out_specs=(P(), P(), P(), P(), P(), P(), P(), P()),
                         check_vma=False)
```

profile of v0, /device:TPU:0, one launch (start us, length us, event | category | flops | bytes accessed | tf_op | source)
XLA Modules:
  0.0 566.1 jit_solution(13999748173314853979)
XLA Ops:
  0.6 1.4 pad_maximum_fusion.vec_ref
  2.0 181.9 %shard_map.152 = (f32[2048,2048]{1,0:T(8,128)}, bf16[2048,2048]{1,0:T(8,128)(2,1)}, f32[2048,2048]{1,0:T(8,128)}, bf16[2048,2048]{1,0:T(8,128)(2,1)}, bf16[2048,...) custom-call(bf16[1024,512]{1,0:T(8,128)(2,1)} %ha_hbm.1, ...), custom_call_target="tpu_custom_call" | custom-call | flops 49999998976 | bytes 125829120 | tf_op jit(solution)/shard_map/pallas_call | solution.py:390
  183.9 353.7 %shard_map.153 = (f32[36,2048,128]{2,1,0:T(8,128)}, f32[36,2048,128]{2,1,0:T(8,128)}, f32[2,4,2048]{2,1,0:T(4,128)}, f32[1,128]{1,0:T(1,128)}) custom-call(bf16[2048,2048]{1,0:T(8,128)(2,1)} %get-tuple-element.26.z_hbm, bf16[2048,2048]{1,0:T(8,128)(2,1)} %get-tuple-element.27.zo_hbm, bf16[2048,2048]{1,0:T(8,128)(2,1)} %get-tuple-element.28.gh_hbm, ...), custom_call_target="tpu_custom_call" | custom-call | flops 149999992832 | bytes 209715200 | tf_op jit(solution)/shard_map/pallas_call | solution.py:739
  537.6 1.5 fusion
  539.1 0.0 copy-start
  539.1 25.9 %shard_map.154 = (f32[512,2048]{1,0:T(8,128)}, f32[2048,2048]{1,0:T(8,128)}, f32[2048,2048]{1,0:T(8,128)}) custom-call(f32[36,2048,128]{2,1,0:T(8,128)} %get-tuple-element.39.groups), custom_call_target="tpu_custom_call" | custom-call | bytes 75497472 | tf_op jit(solution)/shard_map/pallas_call | solution.py:798
  565.0 0.0 copy-done
Async XLA Ops:
  539.1 25.9 %copy-start = (f32[1,128]{1,0:T(1,128)S(1)}, f32[1,128]{1,0:T(1,128)}, u32[]{:S(2)}) copy-start(f32[1,128]{1,0:T(1,128)} %get-tuple-element.38) | copy-start | bytes 1540
where the time goes:
time: 567 us; the launch traced here: 566 us
  Pallas kernels  561 us (99%)
    pallas_call x1, Pallas kernels, backward(): pl.pallas_call(functools.partial(backward_kernel, all_rows), out_shape=(j...  354 us
    pallas_call x1, Pallas kernels, front(): pl.pallas_call(functools.partial(front_kernel, all_rows), out_shape=(shap...  182 us
    pallas_call x1, Pallas kernels, join(): pl.pallas_call(join_kernel, out_shape=(jax.ShapeDtypeStruct((512, dim), F...  25.9 us

commit v1 on v0

--- a/solution.py
+++ b/solution.py
@@ -423,9 +423,9 @@
 
 def backward_kernel(all_rows, z_hbm, zo_hbm, gh_hbm, x2t_hbm, x1t_hbm, ht_hbm, w3_hbm, w2_hbm, u2_hbm, u1_hbm,
                     mp_ref, vec2_ref, vec1_ref, lossv_ref,
-                    out_hbm, part_hbm, grads_ref, loss_ref,
-                    buf_a, buf_b, buf_c, ht, sb, wb, zb, ub, ps, own, r0, r1, r2, st, sr, tot, lacc,
-                    ssem, rsem, lsem, dsem, psem, bsem, tsend, trecv):
+                    out_hbm, part_hbm, da_hbm, grads_ref, loss_ref,
+                    buf_a, buf_b, buf_c, ht, sb, wb, zb, ub, db, ps, own, r0, r1, r2, st, sr, tot, lacc,
+                    ssem, rsem, lsem, dsem, psem, bsem, dasem, tsend, trecv):
     idx = lax.axis_index('data')
     c, x, y = idx % 2, (idx // 2) % 2, idx // 4
     bits = (c, x, y)
@@ -534,12 +534,21 @@
         blk = n % 8
         return ((n < 8, (pltpu.make_async_copy(gh_hbm.at[:, blk_ds(blk)], sb.at[slot], dsem.at[0, slot]),
                          pltpu.make_async_copy(zo_hbm.at[:, blk_ds(blk)], zb.at[slot], dsem.at[1, slot]))),
-                (jnp.logical_and(n >= 8, n < 24),
+                (jnp.logical_and(n >= 8, n < 16),
                  (pltpu.make_async_copy(w3_hbm.at[blk_ds(blk), :], wb.at[slot], dsem.at[0, slot]),
                   pltpu.make_async_copy(u2_hbm.at[:, blk_ds(blk)], ub.at[slot], dsem.at[1, slot]))),
-                (jnp.logical_and(n >= 24, n < 40),
+                (jnp.logical_and(n >= 16, n < 24),
+                 (pltpu.make_async_copy(da_hbm.at[blk], db.at[slot], dsem.at[0, slot]),
+                  pltpu.make_async_copy(u2_hbm.at[:, blk_ds(blk)], ub.at[slot], dsem.at[1, slot]))),
+                (jnp.logical_and(n >= 24, n < 32),
                  (pltpu.make_async_copy(w2_hbm.at[blk_ds(blk), :], wb.at[slot], dsem.at[0, slot]),
+                  pltpu.make_async_copy(u1_hbm.at[:, blk_ds(blk)], ub.at[slot], dsem.at[1, slot]))),
+                (jnp.logical_and(n >= 32, n < 40),
+                 (pltpu.make_async_copy(da_hbm.at[blk], db.at[slot], dsem.at[0, slot]),
                   pltpu.make_async_copy(u1_hbm.at[:, blk_ds(blk)], ub.at[slot], dsem.at[1, slot]))))
+
+    def da_write(n):
+        return pltpu.make_async_copy(db.at[n % 2], da_hbm.at[n % 8], dasem.at[n % 2])
 
     def start_streams(n):
         for cond, cps in streams(n):
@@ -555,9 +564,9 @@
 
     def part_writes_one(n):
         tile = 2 * (n - 32)
-        return tuple(pltpu.make_async_copy(ps.at[pl.ds(0, 512), pl.ds(h * LANE, LANE)],
+        return tuple(pltpu.make_async_copy(ps.at[rds((n % 2) * 512, 512), pl.ds(h * LANE, LANE)],
                                            part_hbm.at[32 + (tile + h) // 4, rds(((tile + h) % 4) * 512, 512)],
-                                           psem.at[h]) for h in range(2))
+                                           psem.at[2 * (n % 2) + h]) for h in range(2))
 
     def loop_tiles(count, fn):
         def step(m, carry):
@@ -590,34 +599,48 @@
         loop_tiles(dim // TILE, grad)
         start_all(part_writes(n))
 
-    def d_act(d_ref, u_slot, r, vec_ref, col, slot):
-        dx = nt(d_ref[r, :], wb[slot])
-        nrm = (ub[slot, r, :] - vec_ref[0:1, col]) * vec_ref[1:2, col]
-        act = vec_ref[2:3, col] * nrm + vec_ref[3:4, col]
-        return jnp.where(act > 0.0, dx, 0.0), nrm
+    def normed(r, vec_ref, col, slot):
+        return (ub[slot, r, :] - vec_ref[0:1, col]) * vec_ref[1:2, col]
 
     def piece_stats(n, d_ref, vec_ref, layer, which):
         slot, col = n % 2, blk_ds(n % 8)
         wait_streams(n, which)
-        start_streams(n + 1)
+
+        @pl.when(n % 8 != 7)
+        def _():
+            start_streams(n + 1)
+
+        @pl.when(n % 8 >= 2)
+        def _():
+            da_write(n - 2).wait()
         st[layer, 0:2, col] = jnp.zeros((2, BLK), F32)
 
         def tile(r):
-            da, nrm = d_act(d_ref, slot, r, vec_ref, col, slot)
+            dx = nt(d_ref[r, :], wb[slot])
+            nrm = normed(r, vec_ref, col, slot)
+            da = jnp.where(vec_ref[2:3, col] * nrm + vec_ref[3:4, col] > 0.0, dx, 0.0)
+            db[slot, r, :] = da
             st[layer, 0:1, col] += jnp.sum(da, axis=0, keepdims=True)
             st[layer, 1:2, col] += jnp.sum(da * nrm, axis=0, keepdims=True)
         loop_tiles(rows // TILE, tile)
-
-    def piece_du(n, d_ref, vec_ref, layer, which, du_ref):
+        da_write(n).start()
+
+        @pl.when(n % 8 == 7)
+        def _():
+            da_write(n - 1).wait()
+            da_write(n).wait()
+            start_streams(n + 1)
+
+    def piece_du(n, vec_ref, layer, which, du_ref):
         slot, col = n % 2, blk_ds(n % 8)
         wait_streams(n, which)
         start_streams(n + 1)
+        scale = vec_ref[1:2, col] * vec_ref[2:3, col]
+        mean_da, mean_dan = tot[layer, 0:1, col] / all_rows, tot[layer, 1:2, col] / all_rows
 
         def tile(r):
-            da, nrm = d_act(d_ref, slot, r, vec_ref, col, slot)
-            du = (vec_ref[1:2, col] * vec_ref[2:3, col]) * (
-                da - tot[layer, 0:1, col] / all_rows - nrm * (tot[layer, 1:2, col] / all_rows))
-            du_ref[r, col] = du.astype(BF16)
+            nrm = normed(r, vec_ref, col, slot)
+            du_ref[r, col] = (scale * (db[slot, r, :] - mean_da - nrm * mean_dan)).astype(BF16)
         loop_tiles(rows // TILE, tile)
         return col
 
@@ -642,13 +665,17 @@
 
     big(0).start()
     start_streams(0)
-    big(1).start()
     ht_copy = pltpu.make_async_copy(ht_hbm, ht, bsem.at[3])
-    ht_copy.start()
     lacc[...] = jnp.zeros_like(lacc)
     st[...] = jnp.zeros_like(st)
     meet([peer(d) for d in range(1, 8)])
     big(0).wait()
+    big(1).start()
+    ht_copy.start()
+
+    def dz_at(t):
+        return (jnp.logical_or(t == 0, jnp.logical_or(t == 2, jnp.logical_and(t >= 4, t < 10))),
+                jnp.where(t < 4, t // 2, t - 2))
 
     def tick(it, carry):
         k = it - 1
@@ -659,27 +686,42 @@
         stage(k - 2 * LAG, to_s2)
         stage(k - LAG, to_s1)
 
-        @pl.when(jnp.logical_or(jnp.logical_and(it >= 1, it <= 8), jnp.logical_and(it >= 17, it <= 24)))
+        wrote_dz, dz_piece = dz_at(it - 1)
+
+        @pl.when(wrote_dz)
+        def _():
+            wait_all(part_writes(dz_piece))
+
+        @pl.when(jnp.logical_and(it >= 17, it <= 24))
         def _():
             wait_all(part_writes(it - 1))
 
-        @pl.when(jnp.logical_and(it >= 29, it <= 36))
-        def _():
-            wait_all(part_writes_one(it + 3))
+        @pl.when(jnp.logical_and(it >= 33, it <= 36))
+        def _():
+            wait_all(part_writes_one(2 * it - 34))
+            wait_all(part_writes_one(2 * it - 33))
 
         stage(k, to_s0)
 
-        @pl.when(it < 8)
-        def _():
-            piece_dz(it)
-
-        @pl.when(jnp.logical_and(it >= 8, it < 16))
-        def _():
-            @pl.when(it == 8)
+        has_dz, dz_now = dz_at(it)
+
+        @pl.when(has_dz)
+        def _():
+            piece_dz(dz_now)
+
+        @pl.when(jnp.logical_and(it >= 10, it < 16))
+        def _():
+            @pl.when(it == 10)
             def _():
                 big(2).start()
 
-            piece_stats(it, buf_c, vec2_ref, 0, 1)
+            twice = jnp.logical_or(it == 10, it == 12)
+            first = jnp.where(it == 10, 8, jnp.where(it < 13, it - 1, it))
+
+            def step(n, carry):
+                piece_stats(n, buf_c, vec2_ref, 0, 1)
+                return carry
+            lax.fori_loop(first, first + jnp.where(twice, 2, 1), step, 0)
 
             @pl.when(it == 15)
             def _():
@@ -696,34 +738,34 @@
                 big(2).wait()
                 ht_copy.wait()
 
-            col = piece_du(it, buf_c, vec2_ref, 0, 1, buf_b)
+            col = piece_du(it, vec2_ref, 0, 2, buf_b)
 
             def grad(r):
                 ps[r, :] = jnp.dot(buf_a[r, :], buf_b[:, col], preferred_element_type=F32)
             loop_tiles(dim // TILE, grad)
             start_all(part_writes(it))
 
-        @pl.when(jnp.logical_and(it >= 24, it < 28))
-        def _():
+        @pl.when(jnp.logical_and(it >= 24, it < 32))
+        def _():
+            piece_stats(it, buf_b, vec1_ref, 1, 3)
+
+            @pl.when(it == 31)
+            def _():
+                send_stats(1)
+
+        @pl.when(jnp.logical_and(it >= 32, it < 36))
+        def _():
+            @pl.when(it == 32)
+            def _():
+                finish_stats(1)
+
             def two(m, carry):
-                piece_stats(24 + 2 * (it - 24) + m, buf_b, vec1_ref, 1, 2)
+                n = 2 * it - 32 + m
+                col = piece_du(n, vec1_ref, 1, 4, buf_c)
+                ps[rds((n % 2) * 512, 512), :] = jnp.dot(ht[...], buf_c[:, col], preferred_element_type=F32)
+                start_all(part_writes_one(n))
                 return carry
             lax.fori_loop(0, 2, two, 0)
-
-            @pl.when(it == 27)
-            def _():
-                send_stats(1)
-
-        @pl.when(jnp.logical_and(it >= 28, it < 36))
-        def _():
-            @pl.when(it == 28)
-            def _():
-                finish_stats(1)
-
-            n = it + 4
-            col = piece_du(n, buf_b, vec1_ref, 1, 2, buf_c)
-            ps[0:512, :] = jnp.dot(ht[...], buf_c[:, col], preferred_element_type=F32)
-            start_all(part_writes_one(n))
 
         return carry
 
@@ -739,19 +781,20 @@
     return pl.pallas_call(
         functools.partial(backward_kernel, all_rows),
         out_shape=(jax.ShapeDtypeStruct((GROUPS, dim, LANE), F32), jax.ShapeDtypeStruct((GROUPS, dim, LANE), F32),
+                   jax.ShapeDtypeStruct((8, rows, BLK), F32),
                    jax.ShapeDtypeStruct((2, 4, dim), F32), jax.ShapeDtypeStruct((1, LANE), F32)),
         in_specs=[hbm] * 10 + [vmem] * 4,
-        out_specs=(hbm, hbm, vmem, vmem),
+        out_specs=(hbm, hbm, hbm, vmem, vmem),
         scratch_shapes=[
             pltpu.VMEM((rows, dim), BF16), pltpu.VMEM((rows, dim), BF16), pltpu.VMEM((rows, dim), BF16),
             pltpu.VMEM((feat, rows), BF16),
             pltpu.VMEM((2, dim, BLK), BF16), pltpu.VMEM((2, BLK, dim), BF16), pltpu.VMEM((2, rows, BLK), BF16),
-            pltpu.VMEM((2, rows, BLK), F32), pltpu.VMEM((dim, BLK), F32),
+            pltpu.VMEM((2, rows, BLK), F32), pltpu.VMEM((2, rows, BLK), F32), pltpu.VMEM((dim, BLK), F32),
             pltpu.VMEM((SLOTS, 1024, LANE), F32), pltpu.VMEM((SLOTS, 1024, LANE), F32),
             pltpu.VMEM((2, SLOTS, 256, LANE), F32), pltpu.VMEM((2, SLOTS, 128, LANE), F32),
             pltpu.VMEM((2, 4, dim), F32), pltpu.VMEM((2, 8, 4, dim), F32), pltpu.VMEM((2, 4, dim), F32),
             pltpu.VMEM((1, BLK), F32),
-            dma((10, SLOTS)), dma((10, SLOTS)), dma((3, SLOTS)), dma((2, 2)), dma((2,)), dma((4,)),
+            dma((10, SLOTS)), dma((10, SLOTS)), dma((3, SLOTS)), dma((2, 2)), dma((4,)), dma((4,)), dma((2,)),
             dma((2, 7)), dma((2, 7)),
         ],
         compiler_params=pltpu.CompilerParams(collective_id=2, has_side_effects=True, vmem_limit_bytes=67043328),
@@ -817,7 +860,7 @@
         vec = jnp.stack([gain_one, bias_one, gain_two, bias_two])
         (u1, _, u2, z, z_other, g_hat, x2t, x1t, ht, stat1, stat2, mean_part, loss_vec) = front(
             h_a, h_b, w_one, w_two, w_three, vec, all_rows)
-        groups, _, grads, loss = backward(z, z_other, g_hat, x2t, x1t, ht, w_three, w_two, u2, u1, mean_part, stat2,
+        groups, _, _, grads, loss = backward(z, z_other, g_hat, x2t, x1t, ht, w_three, w_two, u2, u1, mean_part, stat2,
                                           stat1, loss_vec, all_rows)
         d_w1, d_w2, d_w3 = join(groups, dim)
         return (loss[0, 0], d_w1, d_w2, d_w3,

time: 567 us -> 551 us (0.972)
  Pallas kernels: 561 us -> 546 us
    pallas_call x1, Pallas kernels: 354 us -> 338 us  [backward(): pl.pallas_call(functools.partial(backward_kernel, all_rows), out_shape=(j...]
where the time goes in v1:
time: 551 us
  Pallas kernels  546 us (99%)
    pallas_call x1, Pallas kernels, backward(): pl.pallas_call(functools.partial(backward_kernel, all_rows), out_shape=(j...  338 us
    pallas_call x1, Pallas kernels, front(): pl.pallas_call(functools.partial(front_kernel, all_rows), out_shape=(shap...  182 us
    pallas_call x1, Pallas kernels, join(): pl.pallas_call(join_kernel, out_shape=(jax.ShapeDtypeStruct((512, dim), F...  25.9 us

profile of v1, /device:TPU:0, one launch (start us, length us, event | category | flops | bytes accessed | tf_op | source)
XLA Modules:
  0.0 550.7 jit_solution(13829120114828075256)
XLA Ops:
  0.6 1.4 pad_maximum_fusion.vec_ref
  2.0 181.9 %shard_map.152 = (f32[2048,2048]{1,0:T(8,128)}, bf16[2048,2048]{1,0:T(8,128)(2,1)}, f32[2048,2048]{1,0:T(8,128)}, bf16[2048,2048]{1,0:T(8,128)(2,1)}, bf16[2048,...) custom-call(bf16[1024,512]{1,0:T(8,128)(2,1)} %ha_hbm.1, ...), custom_call_target="tpu_custom_call" | custom-call | flops 49999998976 | bytes 125829120 | tf_op jit(solution)/shard_map/pallas_call | solution.py:390
  183.9 338.2 %shard_map.153 = (f32[36,2048,128]{2,1,0:T(8,128)}, f32[36,2048,128]{2,1,0:T(8,128)}, f32[8,2048,256]{2,1,0:T(8,128)}, f32[2,4,2048]{2,1,0:T(4,128)}, f32[1,128]{1,0:T(1,128)}) custom-call(bf16[2048,2048]{1,0:T(8,128)(2,1)} %get-tuple-element.26.z_hbm, bf16[2048,2048]{1,0:T(8,128)(2,1)} %get-tuple-element.27.zo_hbm, ...), custom_call_target="tpu_custom_call" | custom-call | flops 149999992832 | bytes 209715200 | tf_op jit(solution)/shard_map/pallas_call | solution.py:781
  522.1 1.5 fusion
  523.6 0.0 copy-start
  523.6 25.9 %shard_map.154 = (f32[512,2048]{1,0:T(8,128)}, f32[2048,2048]{1,0:T(8,128)}, f32[2048,2048]{1,0:T(8,128)}) custom-call(f32[36,2048,128]{2,1,0:T(8,128)} %get-tuple-element.39.groups), custom_call_target="tpu_custom_call" | custom-call | bytes 75497472 | tf_op jit(solution)/shard_map/pallas_call | solution.py:841
  549.5 0.0 copy-done
Async XLA Ops:
  523.6 25.9 %copy-start = (f32[1,128]{1,0:T(1,128)S(1)}, f32[1,128]{1,0:T(1,128)}, u32[]{:S(2)}) copy-start(f32[1,128]{1,0:T(1,128)} %get-tuple-element.38) | copy-start | bytes 1540

commit v2 on v1

--- a/solution.py
+++ b/solution.py
@@ -674,8 +674,8 @@
     ht_copy.start()
 
     def dz_at(t):
-        return (jnp.logical_or(t == 0, jnp.logical_or(t == 2, jnp.logical_and(t >= 4, t < 10))),
-                jnp.where(t < 4, t // 2, t - 2))
+        return (jnp.logical_or(jnp.logical_or(t == 0, t == 2), jnp.logical_or(t == 4, jnp.logical_and(t >= 6, t < 11))),
+                jnp.where(t < 6, t // 2, t - 3))
 
     def tick(it, carry):
         k = it - 1
@@ -709,14 +709,14 @@
         def _():
             piece_dz(dz_now)
 
-        @pl.when(jnp.logical_and(it >= 10, it < 16))
-        def _():
-            @pl.when(it == 10)
+        @pl.when(jnp.logical_and(it >= 11, it < 16))
+        def _():
+            @pl.when(it == 11)
             def _():
                 big(2).start()
 
-            twice = jnp.logical_or(it == 10, it == 12)
-            first = jnp.where(it == 10, 8, jnp.where(it < 13, it - 1, it))
+            twice = it < 14
+            first = jnp.where(it < 14, 2 * it - 14, it)
 
             def step(n, carry):
                 piece_stats(n, buf_c, vec2_ref, 0, 1)

time: 551 us -> 545 us (0.989)
  Pallas kernels: 546 us -> 540 us
    pallas_call x1, Pallas kernels: 338 us -> 332 us  [backward(): pl.pallas_call(functools.partial(backward_kernel, all_rows), out_shape=(j...]
where the time goes in v2:
time: 545 us; the launch traced here: 544 us
  Pallas kernels  540 us (99%)
    pallas_call x1, Pallas kernels, backward(): pl.pallas_call(functools.partial(backward_kernel, all_rows), out_shape=(j...  332 us
    pallas_call x1, Pallas kernels, front(): pl.pallas_call(functools.partial(front_kernel, all_rows), out_shape=(shap...  182 us
    pallas_call x1, Pallas kernels, join(): pl.pallas_call(join_kernel, out_shape=(jax.ShapeDtypeStruct((512, dim), F...  25.9 us

profile of v2, /device:TPU:0, one launch (start us, length us, event | category | flops | bytes accessed | tf_op | source)
XLA Modules:
  0.0 544.3 jit_solution(17365915892795595499)
XLA Ops:
  0.6 1.4 pad_maximum_fusion.vec_ref
  2.0 181.9 %shard_map.152 = (f32[2048,2048]{1,0:T(8,128)}, bf16[2048,2048]{1,0:T(8,128)(2,1)}, f32[2048,2048]{1,0:T(8,128)}, bf16[2048,2048]{1,0:T(8,128)(2,1)}, bf16[2048,...) custom-call(bf16[1024,512]{1,0:T(8,128)(2,1)} %ha_hbm.1, ...), custom_call_target="tpu_custom_call" | custom-call | flops 49999998976 | bytes 125829120 | tf_op jit(solution)/shard_map/pallas_call | solution.py:390
  183.9 331.8 %shard_map.153 = (f32[36,2048,128]{2,1,0:T(8,128)}, f32[36,2048,128]{2,1,0:T(8,128)}, f32[8,2048,256]{2,1,0:T(8,128)}, f32[2,4,2048]{2,1,0:T(4,128)}, f32[1,128]{1,0:T(1,128)}) custom-call(bf16[2048,2048]{1,0:T(8,128)(2,1)} %get-tuple-element.26.z_hbm, bf16[2048,2048]{1,0:T(8,128)(2,1)} %get-tuple-element.27.zo_hbm, ...), custom_call_target="tpu_custom_call" | custom-call | flops 149999992832 | bytes 209715200 | tf_op jit(solution)/shard_map/pallas_call | solution.py:781
  515.8 1.5 fusion
  517.2 0.0 copy-start
  517.2 25.9 %shard_map.154 = (f32[512,2048]{1,0:T(8,128)}, f32[2048,2048]{1,0:T(8,128)}, f32[2048,2048]{1,0:T(8,128)}) custom-call(f32[36,2048,128]{2,1,0:T(8,128)} %get-tuple-element.39.groups), custom_call_target="tpu_custom_call" | custom-call | bytes 75497472 | tf_op jit(solution)/shard_map/pallas_call | solution.py:841
  543.1 0.0 copy-done
Async XLA Ops:
  517.2 25.9 %copy-start = (f32[1,128]{1,0:T(1,128)S(1)}, f32[1,128]{1,0:T(1,128)}, u32[]{:S(2)}) copy-start(f32[1,128]{1,0:T(1,128)} %get-tuple-element.38) | copy-start | bytes 1540

commit v3 on v2

--- a/solution.py
+++ b/solution.py
@@ -802,8 +802,8 @@
     )(z, zo, gh, x2t, x1t, ht, w3, w2, u2, u1, mp, vec2, vec1, lossv)
 
 
-RING = 16
-AHEAD = 8
+RING = 24
+AHEAD = 14
 
 
 def join_kernel(groups, w1_out, w2_out, w3_out, buf, lsem, ssem):

time: 545 us -> 545 us (level)
  no operation moved by 1% of the time
where the time goes in v3:
time: 545 us; the launch traced here: 544 us
  Pallas kernels  540 us (99%)
    pallas_call x1, Pallas kernels, backward(): pl.pallas_call(functools.partial(backward_kernel, all_rows), out_shape=(j...  332 us
    pallas_call x1, Pallas kernels, front(): pl.pallas_call(functools.partial(front_kernel, all_rows), out_shape=(shap...  182 us
    pallas_call x1, Pallas kernels, join(): pl.pallas_call(join_kernel, out_shape=(jax.ShapeDtypeStruct((512, dim), F...  26.1 us

profile of v3, /device:TPU:0, one launch (start us, length us, event | category | flops | bytes accessed | tf_op | source)
XLA Modules:
  0.0 544.5 jit_solution(15332880138670280038)
XLA Ops:
  0.6 1.4 pad_maximum_fusion.vec_ref
  2.0 181.9 %shard_map.152 = (f32[2048,2048]{1,0:T(8,128)}, bf16[2048,2048]{1,0:T(8,128)(2,1)}, f32[2048,2048]{1,0:T(8,128)}, bf16[2048,2048]{1,0:T(8,128)(2,1)}, bf16[2048,...) custom-call(bf16[1024,512]{1,0:T(8,128)(2,1)} %ha_hbm.1, ...), custom_call_target="tpu_custom_call" | custom-call | flops 49999998976 | bytes 125829120 | tf_op jit(solution)/shard_map/pallas_call | solution.py:390
  183.9 331.8 %shard_map.153 = (f32[36,2048,128]{2,1,0:T(8,128)}, f32[36,2048,128]{2,1,0:T(8,128)}, f32[8,2048,256]{2,1,0:T(8,128)}, f32[2,4,2048]{2,1,0:T(4,128)}, f32[1,128]{1,0:T(1,128)}) custom-call(bf16[2048,2048]{1,0:T(8,128)(2,1)} %get-tuple-element.26.z_hbm, bf16[2048,2048]{1,0:T(8,128)(2,1)} %get-tuple-element.27.zo_hbm, ...), custom_call_target="tpu_custom_call" | custom-call | flops 149999992832 | bytes 209715200 | tf_op jit(solution)/shard_map/pallas_call | solution.py:781
  515.8 1.5 fusion
  517.2 0.0 copy-start
  517.2 26.1 %shard_map.154 = (f32[512,2048]{1,0:T(8,128)}, f32[2048,2048]{1,0:T(8,128)}, f32[2048,2048]{1,0:T(8,128)}) custom-call(f32[36,2048,128]{2,1,0:T(8,128)} %get-tuple-element.39.groups), custom_call_target="tpu_custom_call" | custom-call | bytes 75497472 | tf_op jit(solution)/shard_map/pallas_call | solution.py:841
  543.3 0.0 copy-done
Async XLA Ops:
  517.2 26.1 %copy-start = (f32[1,128]{1,0:T(1,128)S(1)}, f32[1,128]{1,0:T(1,128)}, u32[]{:S(2)}) copy-start(f32[1,128]{1,0:T(1,128)} %get-tuple-element.38) | copy-start | bytes 1540
